TPU v7x, 128 devices: a whole 4x4x4 slice. The times are simulated.
128 devices in a mesh: img: 16 (over y, z), pix: 8 (over x, core).
Axes of the slice: x: 4, y: 4, z: 4, core: 2. Of those that a mesh axis runs over, the one named last changes fastest.
Arguments:
- images: bfloat16 [6144, 16384], P('img', 'pix'), may hold values from -12 to 12
- inverse_noise_scale: float32 [6144], P('img'), may hold values from 0.4 to 4
- projections: bfloat16 [16384, 16384], P('img', 'pix'), may hold values from -1 to 1
- group_search_blocks: int32 [16, 16], P('img'), may hold values from 0 to 127, as said below
- search_list_count: int32 [16], P('img'), may hold values from 12 to 16, as said below
Outputs:
- projection_sums: float32 [16384, 16384], P('img', 'pix')
- log_evidence: float32 [6144], P(('img', 'pix'))
Inputs may be any that keep to these rules, and one draw needn't show every extreme that they name: `group_search_blocks`: each row lists 16 different block ids; block b is owned by index b // 8 of img. Among the first search_list_count[g] entries of row g no owner appears more than 2 times, and in every draw one owner has 2 of its blocks among the first 2 entries of every row. `search_list_count`: some group's count is 16 in every draw.
All inputs are finite; a program needn't handle non-finite values.
Results may differ from a plain program's by a relative error of at most 0.004.
Values may be sent and summed in bfloat16 or wider, within the bound.
A program may use at most 128 MiB of HBM per device.

v0:
```python
import jax
import jax.numpy as jnp
from jax import lax
from jax.sharding import PartitionSpec as P

BLOCK = 128
CAP = 2
MAXL = 16


def on_device(images, inverse_noise_scale, projections, group_search_blocks, search_list_count):
    group_rows, pixels = images.shape
    n_groups = lax.axis_size("img")
    n_shares = lax.axis_size("pix")
    share_rows = group_rows // n_shares
    owned_blocks = projections.shape[0] // BLOCK
    own_index = lax.axis_index("img")
    first_row = lax.axis_index("pix") * share_rows
    everyone = lax.all_gather(images, "img", axis=0, tiled=True).reshape(
        n_groups, group_rows, pixels
    )
    small = jnp.concatenate(
        [
            group_search_blocks.astype(jnp.float32),
            search_list_count[:, None].astype(jnp.float32),
            lax.dynamic_slice_in_dim(inverse_noise_scale, first_row, share_rows)[None],
        ],
        axis=1,
    )
    table = lax.all_gather(small, "img", axis=0, tiled=True)
    every_list = table[:, :MAXL].astype(jnp.int32)
    every_count = table[:, MAXL].astype(jnp.int32)
    scaling = table[:, MAXL + 1 :]
    positions = jnp.arange(MAXL, dtype=jnp.int32)
    slot_ids = jnp.arange(CAP, dtype=jnp.int32)
    live_entry = positions[None, :] < every_count[:, None]
    local_hit = live_entry & (every_list // owned_blocks == own_index)
    slot_rank = jnp.cumsum(local_hit.astype(jnp.int32), axis=1) - 1
    slot_pick = local_hit[:, None, :] & (slot_rank[:, None, :] == slot_ids[None, :, None])
    slot_offset = jnp.sum(jnp.where(slot_pick, every_list[:, None, :] % owned_blocks, 0), axis=2)
    slot_filled = jnp.any(slot_pick, axis=2)
    stacked = projections.reshape(owned_blocks, BLOCK, pixels)
    outgoing = jnp.take(stacked, slot_offset.reshape(-1), axis=0).reshape(
        n_groups, CAP * BLOCK, pixels
    )
    local_scores = jnp.einsum(
        "gif,gsf->gis", everyone, outgoing, preferred_element_type=jnp.float32
    )
    scores = lax.psum_scatter(local_scores, "pix", scatter_dimension=1, tiled=True)
    live = jnp.repeat(slot_filled, BLOCK, axis=1)[:, None, :]
    logits = jnp.where(live, scores * scaling[:, :, None], jnp.float32(-1e30))
    peak = jnp.max(logits, axis=2)
    total = jnp.sum(jnp.where(live, jnp.exp(logits - peak[:, :, None]), 0.0), axis=2)
    stats = lax.all_gather(jnp.stack([peak, total]), "img", axis=0)
    row_peak = jnp.max(stats[:, 0], axis=0)
    row_total = jnp.sum(stats[:, 1] * jnp.exp(stats[:, 0] - row_peak[None]), axis=0)
    evidence = row_peak + jnp.log(row_total)
    evidence_out = lax.dynamic_index_in_dim(evidence, own_index, 0, keepdims=False)
    exponent = jnp.where(live, jnp.exp(logits - row_peak[:, :, None]), 0.0)
    weights = (exponent / row_total[:, :, None]).astype(jnp.bfloat16)
    weights = lax.all_gather(weights, "pix", axis=1, tiled=True)
    arriving = jnp.einsum(
        "gis,gif->gsf", weights, everyone, preferred_element_type=jnp.float32
    ).astype(jnp.bfloat16)
    placement = (
        slot_offset.reshape(-1)[None, :] == jnp.arange(owned_blocks, dtype=jnp.int32)[:, None]
    ) & slot_filled.reshape(-1)[None, :]
    running_total = jnp.dot(
        placement.astype(jnp.bfloat16),
        arriving.reshape(n_groups * CAP, BLOCK * pixels),
        preferred_element_type=jnp.float32,
    )
    return (running_total.reshape(owned_blocks * BLOCK, pixels), evidence_out)


def solution(mesh):
    placed = (P("img", "pix"), P("img"), P("img", "pix"), P("img", None), P("img"))
    return jax.shard_map(
        on_device,
        mesh=mesh,
        in_specs=placed,
        out_specs=(P("img", "pix"), P(("img", "pix"))),
        check_vma=False,
    )
```

profile of v0, /device:TPU:1, one launch (start us, length us, event | category | flops | bytes accessed | tf_op | source)
XLA Modules:
  0.0 353.3 jit_solution(5376012222658015447)
XLA Ops:
  7.2 0.0 copy-start
  7.2 0.0 all-gather.5.cloned.1.call-start
  7.2 0.7 all-gather.5.cloned.1.call-update
  7.9 0.0 reduce-scatter.2.cloned.1.call-start
  8.6 0.7 convert_element_type.26
  9.3 0.0 copy-done
  9.3 0.1 dynamic-slice_bitcast_fusion
  9.3 0.1 maximum_bitcast_fusion
  9.4 18.4 %all-gather.1 = f32[16,1,65]{2,1,0:T(1,128)S(1)} all-gather(f32[1,1,65]{2,1,0:T(1,128)S(1)} %maximum_bitcast_fusion), channel_id=1, replica_groups=mesh['img'=16,'pix'=8] {'img'}, dimensions={0}, use_global_device_ids=true | all-gather | bytes 4420 | tf_op jit(solution)/shard_map/all_gather | solution.py:30
  27.8 0.2 fusion.8
  28.0 0.1 fusion.20
  28.1 0.2 reduce_window_sum.11
  28.3 0.1 select_reduce_fusion.1
  28.4 0.1 copy.35
  28.5 0.1 reshape.83
  28.6 0.1 copy.38
  28.7 0.1 broadcast_in_dim.79
  28.8 9.3 %gather_fusion = bf16[32,128,2048]{2,1,0:T(8,128)(2,1)} fusion(bf16[8,128,2048]{2,1,0:T(8,128)(2,1)} %bitcast.48, s32[1024]{0:T(1024)S(1)} %pad_clamp_fusion), kind=kCustom, calls=%fused_computation | custom fusion | bytes 33554560 | tf_op jit(solution)/shard_map/jit(_take)/gather | solution.py:43
  38.1 14.3 %bitcast_select_fusion = bf16[16,256,2048]{2,1,0:T(8,128)(2,1)} fusion(pred[16,256]{1,0:T(8,128)(4,1)S(1)} %bitcast.64, bf16[16,256,2048]{2,1,0:T(8,128)(2,1)} %bitcast.47), kind=kLoop, calls=%fused_computation.1 | loop fusion | flops 8388608 | bytes 33558528 | tf_op jit(solution)/shard_map/jit(_take)/select_n | solution.py:43
  52.4 115.0 %all-gather.5.cloned.1.call-done = bf16[6144,2048]{1,0:T(8,128)(2,1)} async-done(((bf16[384,2048]{1,0:T(8,128)(2,1)}), bf16[6144,2048]{1,0:T(8,128)(2,1)}) %all-gather.5.cloned.1.call-update) | async-done | bytes 25165840 | tf_op jit(solution)/shard_map/all_gather | solution.py:19
  167.5 18.7 %convolution_bitcast_fusion = f32[16,384,256]{1,2,0:T(8,128)} fusion(bf16[16,256,2048]{2,1,0:T(8,128)(2,1)} %bitcast_select_fusion, bf16[16,384,2048]{2,1,0:T(8,128)(2,1)} %bitcast.49), kind=kOutput, calls=%fused_computation.4 | convolution fusion | flops 6442450944 | bytes 48234496 | tf_op jit(solution)/shard_map/gif,gsf->gis/dot_general | solution.py:46
  186.2 6.7 %copy.40 = f32[16,384,256]{2,0,1:T(8,128)} copy(f32[16,384,256]{1,2,0:T(8,128)} %convolution_bitcast_fusion) | data formatting | bytes 12582912 | tf_op jit(solution)/shard_map/gif,gsf->gis/dot_general | solution.py:46
  192.9 0.0 reduce-scatter.2.cloned.1.call-update
  192.9 0.0 all-gather.7.cloned.1.call-start
  193.0 0.1 slice.25
  193.0 0.1 fusion.6
  193.1 0.1 copy.36
  193.3 0.1 broadcast_in_dim.76
  193.4 0.1 copy.41
  193.4 41.3 %reduce-scatter.2.cloned.1.call-done = f32[16,48,256]{2,0,1:T(8,128)} async-done(((f32[16,384,256]{2,0,1:T(8,128)}), f32[16,48,256]{2,0,1:T(8,128)}) %reduce-scatter.2.cloned.1.call-update) | async-done | bytes 786448 | tf_op jit(solution)/shard_map/reduce_scatter | solution.py:49
  234.7 1.4 fusion.1
  236.2 1.5 select_reduce_fusion
  237.7 0.1 copy.43
  237.8 0.1 copy.42
  237.8 18.9 %all-gather = f32[32,16,48]{2,1,0:T(8,128)S(1)} all-gather(f32[2,16,48]{2,1,0:T(8,128)S(1)} %pad_maximum_fusion), channel_id=2, replica_groups=mesh['img'=16,'pix'=8] {'img'}, dimensions={0}, use_global_device_ids=true | all-gather | bytes 104448 | tf_op jit(solution)/shard_map/all_gather | solution.py:54
  256.8 0.1 copy.45
  256.9 0.1 copy.46
  257.0 2.3 divide_convert_fusion
  259.3 0.0 all-gather.7.cloned.1.call-update
  259.3 0.1 and.47
  259.4 0.1 eq.41
  259.5 0.5 fusion.19
  260.0 30.4 %all-gather.7.cloned.1.call-done = bf16[16,384,256]{2,0,1:T(8,128)(2,1)} async-done(((bf16[16,48,256]{2,0,1:T(8,128)(2,1)}), bf16[16,384,256]{2,0,1:T(8,128)(2,1)}) %all-gather.7.cloned.1.call-update) | async-done | bytes 3145744 | tf_op jit(solution)/shard_map/all_gather | solution.py:61
  290.4 21.9 %convolution_convert_fusion = bf16[16,256,2048]{2,1,0:T(8,128)(2,1)} fusion(bf16[16,384,2048]{2,1,0:T(8,128)(2,1)} %bitcast.50, bf16[16,384,256]{2,0,1:T(8,128)(2,1)} %all-gather.7.cloned.1.call-done), kind=kOutput, calls=%fused_computation.2 | convolution fusion | flops 6450839552 | bytes 45088768 | tf_op jit(solution)/shard_map/gis,gif->gsf/dot_general | solution.py:62
  312.3 14.9 %reshape.85 = bf16[32,262144]{1,0:T(8,128)(2,1)} reshape(bf16[16,256,2048]{2,1,0:T(8,128)(2,1)} %convolution_convert_fusion) | data formatting | bytes 33554432 | tf_op jit(solution)/shard_map/reshape | solution.py:70
  327.2 11.3 %fusion.14 = f32[8,262144]{1,0:T(8,128)} fusion(bf16[32,262144]{1,0:T(8,128)(2,1)} %reshape.85, s32[32]{0:T(128)S(1)} %eq.41, pred[32]{0:T(512)(128)(4,1)S(1)} %and.47), kind=kOutput, calls=%fused_computation.41 | convolution fusion | flops 134218240 | bytes 25165984 | tf_op jit(solution)/shard_map/dot_general | solution.py:68
  338.5 8.3 %reshape.86 = f32[1024,2048]{1,0:T(8,128)} reshape(f32[8,262144]{1,0:T(8,128)} %fusion.14) | data formatting | bytes 16777216 | tf_op jit(solution)/shard_map/reshape | solution.py:73
  346.8 0.0 copy-done.1
  (10 shorter events, 0.1 us)
Async XLA Ops:
  7.2 2.1 copy-start
  7.2 160.3 %all-gather.5.cloned.1.call-start = ((), (), s32[]{:S(2)}) async-start(), calls=%async_computation.1 | async-start | bytes 26738688 | tf_op jit(solution)/shard_map/all_gather | solution.py:19
  7.9 226.8 %reduce-scatter.2.cloned.1.call-start = ((), (), s32[]{:S(2)}) async-start(), calls=%async_computation.2 | async-start | bytes 7077888 | tf_op jit(solution)/shard_map/reduce_scatter | solution.py:49
  192.9 97.5 %all-gather.7.cloned.1.call-start = ((), (), s32[]{:S(2)}) async-start(), calls=%async_computation.3 | async-start | bytes 3538944 | tf_op jit(solution)/shard_map/all_gather | solution.py:61
  312.3 34.5 %copy-start.1 = (f32[384]{0:T(512)S(1)}, f32[384]{0:T(512)}, u32[]{:S(2)}) copy-start(f32[384]{0:T(512)} %param.6) | copy-start | bytes 4612
Sparse Core Ops, SparseCore 0:
  10.2 157.2 all-gather.4
  193.0 41.6 reduce-scatter.1
  259.4 30.9 all-gather.6
where the time goes:
time: 354 us; the launch traced here: 353 us
  waiting for transfers between devices  187 us (53%)
  matrix products  51.9 us (15%)
  local copies, waits for them, and re-layouts  40.5 us (11%)
  blocking collectives  37.3 us (11%)
  other arithmetic  21.5 us (6%)
  between operations  14.5 us (4%)
    all_gather x1, waiting for transfers between devices, on_device(): lax.all_gather(images, 'img', axis=0, tiled=True)  115 us
    reduce_scatter x1, waiting for transfers between devices, on_device(): lax.psum_scatter(local_scores, 'pix', scatter_dimension=1, tiled=True)  41.3 us
    all_gather x1, waiting for transfers between devices, on_device(): weights = lax.all_gather(weights, 'pix', axis=1, tiled=True)  30.4 us
    dot_general x1, matrix products, on_device(): jnp.einsum('gis,gif->gsf', weights, everyone, preferred_element_type=jnp....  21.9 us
    all_gather x1, blocking collectives, on_device(): stats = lax.all_gather(jnp.stack([peak, total]), 'img', axis=0)  18.9 us
    dot_general x1, matrix products, on_device(): jnp.einsum('gif,gsf->gis', everyone, outgoing, preferred_element_type=jnp...  18.7 us
    all_gather x1, blocking collectives, on_device(): table = lax.all_gather(small, 'img', axis=0, tiled=True)  18.4 us
    reshape x1, local copies, waits for them, and re-layouts, on_device(): arriving.reshape(n_groups * CAP, BLOCK * pixels)  14.9 us
  transfers between devices with their start and end apart: 3, of which 3 were waited for; matrix products, arithmetic and copies ran while one was open for 8% of the time, Pallas kernels for 0%

commit v1 on v0

--- a/solution.py
+++ b/solution.py
@@ -16,9 +16,9 @@
     owned_blocks = projections.shape[0] // BLOCK
     own_index = lax.axis_index("img")
     first_row = lax.axis_index("pix") * share_rows
-    everyone = lax.all_gather(images, "img", axis=0, tiled=True).reshape(
-        n_groups, group_rows, pixels
-    )
+    everyone = jnp.concatenate(
+        lax.all_to_all(jnp.stack([images] * lax.axis_size("img")), "img", 0, 0), axis=0
+    ).reshape(n_groups, group_rows, pixels)
     small = jnp.concatenate(
         [
             group_search_blocks.astype(jnp.float32),

time: 354 us -> 710 us (2.01)
  blocking collectives: 37.3 us -> 486 us
  waiting for transfers between devices: 187 us -> 77.6 us
  local copies, waits for them, and re-layouts: 40.5 us -> 50.1 us
  starting transfers between devices: 0.12 us -> 8.85 us
    all_gather x1, blocking collectives: 18.4 us -> 467 us  [on_device(): table = lax.all_gather(small, 'img', axis=0, tiled=True)]
    all_gather x1 -> x0, waiting for transfers between devices: 115 us -> none  [on_device(): lax.all_gather(images, 'img', axis=0, tiled=True)]
    another operation x0 -> x1, local copies, waits for them, and re-layouts: none -> 9.57 us  [on_device(): jnp.stack([images] * lax.axis_size('img'))]
    all_to_all x0 -> x1, starting transfers between devices: none -> 8.76 us  [on_device(): lax.all_to_all(jnp.stack([images] * lax.axis_size('img')), 'img', 0, 0)]
  transfers between devices with their start and end apart: 3 -> 3, of which waited for: 3 -> 2; matrix products, arithmetic and copies ran while one was open for 8% -> 4% of each run, Pallas kernels for 0% -> 0%
where the time goes in v1:
time: 710 us
  blocking collectives  486 us (68%)
  waiting for transfers between devices  77.6 us (11%)
  matrix products  51.9 us (7%)
  local copies, waits for them, and re-layouts  50.1 us (7%)
  other arithmetic  20.8 us (3%)
  between operations  14.8 us (2%)
  starting transfers between devices  8.85 us (1%)
    all_gather x1, blocking collectives, on_device(): table = lax.all_gather(small, 'img', axis=0, tiled=True)  467 us
    reduce_scatter x1, waiting for transfers between devices, on_device(): lax.psum_scatter(local_scores, 'pix', scatter_dimension=1, tiled=True)  47.1 us
    all_gather x1, waiting for transfers between devices, on_device(): weights = lax.all_gather(weights, 'pix', axis=1, tiled=True)  30.4 us
    dot_general x1, matrix products, on_device(): jnp.einsum('gis,gif->gsf', weights, everyone, preferred_element_type=jnp....  21.9 us
    all_gather x1, blocking collectives, on_device(): stats = lax.all_gather(jnp.stack([peak, total]), 'img', axis=0)  18.9 us
    dot_general x1, matrix products, on_device(): jnp.einsum('gif,gsf->gis', everyone, outgoing, preferred_element_type=jnp...  18.7 us
    reshape x1, local copies, waits for them, and re-layouts, on_device(): arriving.reshape(n_groups * CAP, BLOCK * pixels)  14.9 us
  transfers between devices with their start and end apart: 3, of which 2 were waited for; matrix products, arithmetic and copies ran while one was open for 4% of the time, Pallas kernels for 0%

profile of v1, /device:TPU:1, one launch (start us, length us, event | category | flops | bytes accessed | tf_op | source)
XLA Modules:
  0.0 709.6 jit_solution(13240052928875503686)
XLA Ops:
  7.2 0.0 copy-start
  7.2 9.6 %stack.8 = bf16[16,384,2048]{2,1,0:T(8,128)(2,1)} broadcast(bf16[384,2048]{1,0:T(8,128)(2,1)} %param.5), dimensions={1,2} | broadcast | bytes 26738688 | tf_op jit(solution)/shard_map/stack | solution.py:20
  16.8 8.8 %all-to-all-start = ((bf16[16,384,2048]{2,1,0:T(8,128)(2,1)}), bf16[16,384,2048]{2,1,0:T(8,128)(2,1)}, u32[]{:S(2)}, u32[]{:S(2)}) async-start(bf16[16,384,2048]{2,1,0:T(8,128)(2,1)} %stack.8), calls=%async_computation | async-start | bytes 50331648 | tf_op jit(solution)/shard_map/all_to_all | solution.py:20
  25.5 0.0 reduce-scatter.2.cloned.1.call-start
  26.2 0.0 copy-done.2
  26.2 0.0 copy-done
  26.3 0.1 dynamic-slice_bitcast_fusion
  26.3 0.1 maximum_bitcast_fusion
  26.4 466.7 %all-gather.1 = f32[16,1,65]{2,1,0:T(1,128)S(1)} all-gather(f32[1,1,65]{2,1,0:T(1,128)S(1)} %maximum_bitcast_fusion), channel_id=1, replica_groups=mesh['img'=16,'pix'=8] {'img'}, dimensions={0}, use_global_device_ids=true | all-gather | bytes 4420 | tf_op jit(solution)/shard_map/all_gather | solution.py:30
  493.1 0.2 fusion.8
  493.3 0.1 fusion.20
  493.4 0.2 reduce_window_sum.11
  493.6 0.1 select_reduce_fusion.1
  493.7 0.1 copy.35
  493.8 0.1 copy.38
  493.9 0.1 broadcast_in_dim.79
  494.0 0.1 reshape.82
  494.1 9.3 %gather_fusion = bf16[32,128,2048]{2,1,0:T(8,128)(2,1)} fusion(bf16[8,128,2048]{2,1,0:T(8,128)(2,1)} %bitcast.47, s32[1024]{0:T(1024)S(1)} %pad_clamp_fusion), kind=kCustom, calls=%fused_computation | custom fusion | bytes 33554560 | tf_op jit(solution)/shard_map/jit(_take)/gather | solution.py:43
  503.5 14.2 %bitcast_select_fusion = bf16[16,256,2048]{2,1,0:T(8,128)(2,1)} fusion(pred[16,256]{1,0:T(8,128)(4,1)S(1)} %bitcast.61, bf16[16,256,2048]{2,1,0:T(8,128)(2,1)} %bitcast.46), kind=kLoop, calls=%fused_computation.1 | loop fusion | flops 8388608 | bytes 33558528 | tf_op jit(solution)/shard_map/jit(_take)/select_n | solution.py:43
  517.6 0.0 all-to-all-done
  517.6 18.7 %convolution_bitcast_fusion = f32[16,384,256]{1,2,0:T(8,128)} fusion(bf16[16,256,2048]{2,1,0:T(8,128)(2,1)} %bitcast_select_fusion, bf16[16,384,2048]{2,1,0:T(8,128)(2,1)} %all-to-all-done), kind=kOutput, calls=%fused_computation.4 | convolution fusion | flops 6442450944 | bytes 48234496 | tf_op jit(solution)/shard_map/gif,gsf->gis/dot_general | solution.py:46
  536.4 6.7 copy.40
  543.0 0.0 reduce-scatter.2.cloned.1.call-update
  543.1 0.0 all-gather.4.cloned.1.call-start
  543.1 0.1 slice.25
  543.2 0.1 copy.41
  543.3 0.1 fusion.6
  543.4 0.1 copy.36
  543.5 0.1 broadcast_in_dim.76
  543.6 47.1 %reduce-scatter.2.cloned.1.call-done = f32[16,48,256]{2,0,1:T(8,128)} async-done(((f32[16,384,256]{2,0,1:T(8,128)}), f32[16,48,256]{2,0,1:T(8,128)}) %reduce-scatter.2.cloned.1.call-update) | async-done | bytes 786448 | tf_op jit(solution)/shard_map/reduce_scatter | solution.py:49
  590.7 1.4 fusion.1
  592.2 1.5 select_reduce_fusion
  593.7 0.1 copy.43
  593.8 0.1 copy.42
  593.8 18.9 %all-gather = f32[32,16,48]{2,1,0:T(8,128)S(1)} all-gather(f32[2,16,48]{2,1,0:T(8,128)S(1)} %pad_maximum_fusion), channel_id=2, replica_groups=mesh['img'=16,'pix'=8] {'img'}, dimensions={0}, use_global_device_ids=true | all-gather | bytes 104448 | tf_op jit(solution)/shard_map/all_gather | solution.py:54
  612.8 0.1 copy.45
  612.9 0.1 copy.46
  613.0 2.3 divide_convert_fusion
  615.3 0.0 all-gather.4.cloned.1.call-update
  615.3 0.1 eq.41
  615.4 0.1 and.47
  615.5 0.5 fusion.19
  616.0 30.4 %all-gather.4.cloned.1.call-done = bf16[16,384,256]{2,0,1:T(8,128)(2,1)} async-done(((bf16[16,48,256]{2,0,1:T(8,128)(2,1)}), bf16[16,384,256]{2,0,1:T(8,128)(2,1)}) %all-gather.4.cloned.1.call-update) | async-done | bytes 3145744 | tf_op jit(solution)/shard_map/all_gather | solution.py:61
  646.4 21.9 %convolution_convert_fusion = bf16[16,256,2048]{2,1,0:T(8,128)(2,1)} fusion(bf16[16,384,2048]{2,1,0:T(8,128)(2,1)} %all-to-all-done, bf16[16,384,256]{2,0,1:T(8,128)(2,1)} %all-gather.4.cloned.1.call-done), kind=kOutput, calls=%fused_computation.2 | convolution fusion | flops 6450839552 | bytes 45088768 | tf_op jit(solution)/shard_map/gis,gif->gsf/dot_general | solution.py:62
  668.3 14.9 %reshape.83 = bf16[32,262144]{1,0:T(8,128)(2,1)} reshape(bf16[16,256,2048]{2,1,0:T(8,128)(2,1)} %convolution_convert_fusion) | data formatting | bytes 33554432 | tf_op jit(solution)/shard_map/reshape | solution.py:70
  683.2 11.3 %fusion.14 = f32[8,262144]{1,0:T(8,128)} fusion(bf16[32,262144]{1,0:T(8,128)(2,1)} %reshape.83, s32[32]{0:T(128)S(1)} %eq.41, pred[32]{0:T(512)(128)(4,1)S(1)} %and.47), kind=kOutput, calls=%fused_computation.41 | convolution fusion | flops 134218240 | bytes 25165984 | tf_op jit(solution)/shard_map/dot_general | solution.py:68
  694.5 8.3 %reshape.84 = f32[1024,2048]{1,0:T(8,128)} reshape(f32[8,262144]{1,0:T(8,128)} %fusion.14) | data formatting | bytes 16777216 | tf_op jit(solution)/shard_map/reshape | solution.py:73
  702.8 0.0 copy-done.1
  (12 shorter events, 0.1 us)
Async XLA Ops:
  7.2 19.1 %copy-start = (f32[384]{0:T(512)S(1)}, f32[384]{0:T(512)}, u32[]{:S(2)}) copy-start(f32[384]{0:T(512)} %param.6) | copy-start | bytes 4612
  16.8 9.5 %copy-start.2 = (s32[1,16]{1,0:T(1,128)S(1)}, s32[1,16]{1,0:T(1,128)}, u32[]{:S(2)}) copy-start(s32[1,16]{1,0:T(1,128)} %param.8) | copy-start | bytes 196
  16.8 500.9 %all-to-all-start = ((bf16[16,384,2048]{2,1,0:T(8,128)(2,1)}), bf16[16,384,2048]{2,1,0:T(8,128)(2,1)}, u32[]{:S(2)}, u32[]{:S(2)}) async-start(bf16[16,384,2048]{2,1,0:T(8,128)(2,1)} %stack.8), calls=%async_computation | async-start | bytes 50331648 | tf_op jit(solution)/shard_map/all_to_all | solution.py:20
  25.5 565.2 %reduce-scatter.2.cloned.1.call-start = ((), (), s32[]{:S(2)}) async-start(), calls=%async_computation.2 | async-start | bytes 7077888 | tf_op jit(solution)/shard_map/reduce_scatter | solution.py:49
  543.1 103.4 %all-gather.4.cloned.1.call-start = ((), (), s32[]{:S(2)}) async-start(), calls=%async_computation.3 | async-start | bytes 3538944 | tf_op jit(solution)/shard_map/all_gather | solution.py:61
  668.3 34.5 %copy-start.1 = (f32[384]{0:T(512)S(1)}, f32[384]{0:T(512)}, u32[]{:S(2)}) copy-start(f32[384]{0:T(512)} %param.6) | copy-start | bytes 4612
Sparse Core Ops, SparseCore 0:
  543.2 47.5 reduce-scatter.1
  615.4 30.9 all-gather.3
